TPU v7x, 512 devices: a whole 4x8x8 slice. The times are simulated.
512 devices in a mesh: row: 16 (over y, core), col: 32 (over z, x).
Axes of the slice: x: 4, y: 8, z: 8, core: 2. Of those that a mesh axis runs over, the one named last changes fastest.
Arguments:
- offsets: float32 [3, 131072], P(None, ('row', 'col')), may hold values from 0 to 11
- cells: int32 [3, 1024], replicated, may hold values from 0 to 15, as said below
- types: int32 [131072], P(('row', 'col')), may hold values from 0 to 3, as said below
- mask: int32 [16, 64, 16, 64], P(None, 'col', 'row'), may hold values from 0 to 1, as said below
- chi_table: float32 [4], replicated, may hold values from 2 to 10.1
- eta_table: float32 [4], replicated, may hold values from 13 to 18
- gamma_table: float32 [4], replicated, may hold values from 0.4 to 0.8
Outputs:
- charges: float32 [131072], P(('row', 'col'))
Inputs may be any that keep to these rules, and one draw needn't show every extreme that they name: The cells of the blocks are a permutation of all 16 x 16 x 4 cells: each cell holds exactly one block. The mask marks a pair of blocks exactly when their cells are equal or adjacent on the periodic grid in every dimension; it is symmetric and each block is marked with exactly 27 blocks, itself included. `types`: types 2 and 3 grow more common along the atoms, from none in the first 256 atoms to nearly all in the last.
All inputs are finite; a program needn't handle non-finite values.
Results may differ from a plain program's by a relative error of at most 0.0003.
Values sent between devices are 32-bit elements; how exact they have to be, the bound alone decides.
A program may use at most 64 MiB of HBM per device.

v0:
```python
import jax
import jax.numpy as jnp
from jax import lax
from jax.sharding import Mesh
from jax.sharding import PartitionSpec as P

BLOCK = 128
GRID_Z = 4
ITERS = 3
ROW_COL = ("row_0", "row_1", "col_0", "col_1")
ROW = ("row_0", "row_1")
COL = ("col_0", "col_1")
coulomb = 14.4
cutoff = 10.0
cell_side = 11.0
pair_group = 64


def copy_for_each(value, axis):
    devices = lax.axis_size(axis)
    return lax.all_to_all(
        jnp.broadcast_to(value[None], (devices, *value.shape)), axis, 0, 0, tiled=True
    )


def over_copies(value, axis):
    return copy_for_each(value, axis).sum(axis=0)


def over_axes(value, axes):
    far, near = axes
    return over_copies(over_copies(value, near), far)


def in_one(arrays, axis):
    line, at, outs = (jnp.concatenate([a.reshape(-1) for a in arrays]), 0, [])
    subtotal = over_axes(line, axis)
    for a in arrays:
        outs.append(subtotal[at : at + a.size].reshape(a.shape))
        at += a.size
    return tuple(outs)


def in_order(blocks, dim):
    blocks = jnp.moveaxis(blocks, 0, dim)
    lengths = blocks.shape
    return blocks.reshape(*lengths[:dim], lengths[dim] * lengths[dim + 1], *lengths[dim + 2 :])


def gathered_copies(value, axis, dim):
    return in_order(copy_for_each(value, axis), dim)


def in_blocks(value, dim, devices):
    before, after = (value.shape[:dim], value.shape[dim + 1 :])
    return jnp.moveaxis(value.reshape(*before, devices, -1, *after), dim, 0)


def sent_and_summed(value, axis, dim):
    devices = lax.axis_size(axis)
    blocks = lax.all_to_all(in_blocks(value, dim, devices), axis, 0, 0, tiled=True)
    return jnp.sum(blocks, axis=0)


def taper(dist):
    xval = dist / cutoff
    poly = 1.0 + xval**4 * (-35.0 + xval * (84.0 + xval * (-70.0 + 20.0 * xval)))
    return jnp.where(xval < 1.0, poly, 0.0)


def coupling(tgt, src, tgt_cell, src_cell, same, grid):
    half = grid[:, None] // 2
    shift = ((src_cell - tgt_cell + half) % grid[:, None] - half).astype(jnp.float32) * cell_side
    radius_sq = jnp.zeros((tgt.shape[1], tgt.shape[2], src.shape[2]), jnp.float32)
    for comp in range(3):
        delta = shift[comp][:, None, None] + src[comp][:, None, :] - tgt[comp][:, :, None]
        radius_sq = radius_sq + delta * delta
    dist = jnp.sqrt(radius_sq)
    paired = tgt[3][:, :, None] * src[3][:, None, :]
    shield = 1.0 / (paired * jnp.sqrt(paired))
    kern = coulomb * taper(dist) / jnp.cbrt(radius_sq * dist + shield)
    width = tgt.shape[2]
    diag = jnp.arange(width)[:, None] == jnp.arange(width)[None, :]
    return jnp.where(same[:, None, None] & diag[None], 0.0, kern)


def pick(kinds, table):
    return jnp.sum(jnp.where(kinds, table[:, None], 0.0), axis=0)


def paired_sums(residual, image):
    return in_one(
        (jnp.sum(residual * residual, axis=1), jnp.sum(residual * image, axis=1)),
        ("row_0", ("row_1", "col_0", "col_1")),
    )


def per_device(offsets, cells, types, mask, chi_table, eta_table, gamma_table):
    n_row = lax.axis_size(ROW)
    n_col = lax.axis_size(COL)
    row_at = lax.axis_index(ROW)
    col_at = lax.axis_index(COL)
    span = types.shape[0]
    bpd = span // BLOCK
    n_tgt = n_row * bpd
    n_src = n_col * bpd
    grid = jnp.array([n_row, n_src // GRID_Z, GRID_Z], jnp.int32)
    kinds = jnp.arange(chi_table.shape[0])[:, None] == types[None, :]
    chi = pick(kinds, chi_table)
    eta = pick(kinds, eta_table)
    gamma = pick(kinds, gamma_table)
    geo = jnp.concatenate([offsets, gamma[None]], axis=0)
    src_geo = gathered_copies(geo, COL, 1).reshape(4, n_src, BLOCK)
    tgt_geo = lax.all_gather(geo, ROW, axis=1, tiled=True).reshape(4, n_tgt, BLOCK)
    tgt_ids = (
        (jnp.arange(n_row, dtype=jnp.int32)[:, None] * n_col + col_at) * bpd
        + jnp.arange(bpd, dtype=jnp.int32)[None, :]
    ).reshape(n_tgt)
    src_ids = row_at * n_src + jnp.arange(n_src, dtype=jnp.int32)
    tgt_cells = jnp.take(cells, tgt_ids, axis=1)
    src_cells = jnp.take(cells, src_ids, axis=1)
    tile = mask.reshape(n_tgt * n_src)
    count = jnp.sum(tile)
    slots = jnp.nonzero(tile, size=n_tgt * n_src + pair_group, fill_value=0)[0].astype(jnp.int32)
    groups = (count + pair_group - 1) // pair_group
    src_range = jnp.arange(n_src, dtype=jnp.int32)

    def block_kernel(step):
        picked = lax.dynamic_slice_in_dim(slots, step * pair_group, pair_group)
        live = step * pair_group + jnp.arange(pair_group) < count
        tgt_blk = picked // n_src
        src_blk = picked % n_src
        kern = coupling(
            tgt_geo[:, tgt_blk],
            src_geo[:, src_blk],
            tgt_cells[:, tgt_blk],
            src_cells[:, src_blk],
            tgt_ids[tgt_blk] == src_ids[src_blk],
            grid,
        )
        return (jnp.where(live[:, None, None], kern, 0.0), tgt_blk, src_blk)

    def apply(direction):
        remote = lax.all_gather(direction, ROW, axis=1, tiled=True).reshape(2, n_tgt, BLOCK)

        def turn(step, acc):
            kern, tgt_blk, src_blk = block_kernel(step)
            contrib = jnp.einsum(
                "gij,kgi->kgj", kern, remote[:, tgt_blk], precision=lax.Precision.HIGHEST
            )
            owners = (src_range[:, None] == src_blk[None, :]).astype(jnp.float32)
            return acc + jnp.einsum("sg,kgj->ksj", owners, contrib, precision=lax.Precision.HIGHEST)

        acc = lax.fori_loop(0, groups, turn, jnp.zeros((2, n_src, BLOCK), jnp.float32))
        summed = sent_and_summed(acc.reshape(2, n_src * BLOCK), COL, 1)
        return summed + eta[None] * direction

    rhs = jnp.stack([-chi, -jnp.ones_like(chi)], axis=0)
    solution = jnp.zeros_like(rhs)
    residual = rhs
    image = apply(residual)
    norm_now, product = paired_sums(residual, image)
    alpha = norm_now / product
    direction = residual
    along = image
    for step in range(ITERS):
        solution = solution + alpha[:, None] * direction
        residual = residual - alpha[:, None] * along
        if step + 1 < ITERS:
            image = apply(residual)
            norm_next, product = paired_sums(residual, image)
            ratio = norm_next / norm_now
            alpha = norm_next / (product - ratio * norm_next / alpha)
            direction = residual + ratio[:, None] * direction
            along = image + ratio[:, None] * along
            norm_now = norm_next
    totals = over_axes(jnp.sum(solution, axis=1), ("row_0", ("row_1", "col_0", "col_1")))
    return solution[0] - totals[0] / totals[1] * solution[1]


def solution(mesh):
    torus = Mesh(mesh.devices.reshape(8, 2, 8, 4), ("row_0", "row_1", "col_0", "col_1"))
    placed = (P(None, ROW_COL), P(), P(ROW_COL), P(None, COL, ROW, None), P(), P(), P())
    return jax.shard_map(
        per_device, mesh=torus, in_specs=placed, out_specs=P(ROW_COL), check_vma=False
    )
```

profile of v0, /device:TPU:1, one launch (start us, length us, event | category | flops | bytes accessed | tf_op | source)
XLA Modules:
  0.0 372.8 jit_solution(4462579200094896409)
XLA Ops:
  0.0 0.8 select_reduce_fusion
  0.8 0.7 pad_maximum_fusion
  1.5 0.7 broadcast_in_dim.293
  2.2 13.7 %all-to-all-start = ((f32[32,4,256]{2,1,0:T(4,128)}), f32[32,4,256]{2,1,0:T(4,128)S(1)}, u32[]{:S(2)}, u32[]{:S(2)}) async-start(f32[32,4,256]{2,1,0:T(4,128)} %broadcast_in_dim.293), calls=%async_computation | async-start | bytes 262144 | tf_op jit(solution)/shard_map/all_to_all | solution.py:21
  15.9 1.4 fusion.201
  18.5 0.6 gather_fusion.21
  19.1 0.6 gather_fusion.22
  19.8 0.3 reduce-window.16
  20.4 14.7 %scatter_custom_fusion = s32[2112]{0:T(1024)S(1)} fusion(s32[2048]{0:T(1024)S(1)} %bitcast.241, s32[2048]{0:T(1024)S(1)} %broadcast.958, s32[]{:T(128)} %constant.520.clone.1), kind=kCustom, calls=%fused_computation.302 | custom fusion | flops 2048 | bytes 8452 | tf_op jit(solution)/shard_map/scatter-add | solution.py:124
  35.7 18.5 %all_gather.12 = f32[2,4096]{1,0:T(2,128)S(1)} all-gather(f32[2,256]{1,0:T(2,128)S(1)} %stack.2), channel_id=1, replica_groups=mesh['row_0'=8,'row_1'=2,'col_0'=8,'col_1'=4] {'row_0','row_1'}, dimensions={1}, use_global_device_ids=true | all-gather | bytes 34816 | tf_op jit(solution)/shard_map/all_gather | solution.py:144
  54.2 0.7 fusion.199
  54.9 15.1 %all_gather.13 = f32[4,4096]{1,0:T(4,128)S(1)} all-gather(f32[4,256]{1,0:T(4,128)S(1)} %pad_maximum_fusion), channel_id=1, replica_groups=mesh['row_0'=8,'row_1'=2,'col_0'=8,'col_1'=4] {'row_0','row_1'}, dimensions={1}, use_global_device_ids=true | all-gather | bytes 69632 | tf_op jit(solution)/shard_map/all_gather | solution.py:114
  70.1 21.0 %while.48 = (s32[]{:T(128)}, f32[2,64,128]{2,1,0:T(8,128)S(1)}, s32[]{:T(128)}, s32[2112]{0:T(1024)S(1)}, f32[2,32,128]{2,0,1:T(2,128)S(1)}, /*index=5*/s32[]{:T...) while((s32[]{:T(128)}, f32[2,64,128]{2,1,0:T(8,128)S(1)}, ...), condition=%wide.region_11.13_spmd.clone.clone.clone, body=%wide.region_10.12_spmd.sunk.clone.clone.clone.sunk | while | flops 70322144 | bytes 2021583 | solution.py:154
  70.3 0.6 gather_fusion.2
  70.9 0.6 gather_fusion.3
  71.5 0.4 fusion.248
  72.0 0.7 gather_fusion
  73.0 0.8 gather_fusion.5
  74.0 0.8 gather_fusion.4
  74.8 0.7 gather_fusion.1
  75.5 0.7 gather_fusion.6
  76.2 0.6 add_compare_fusion.6
  76.8 14.2 %fusion.249 = f32[2,64,128]{2,0,1:T(2,128)S(1)} fusion(f32[64,128]{1,0:T(8,128)S(1)} %bitcast.216, f32[64,128]{1,0:T(8,128)S(1)} %bitcast.222, f32[64,128]{1,0:T(8,128)S(1)} %bitcast.220, f32[64,128]{1,0:T(8,128)S(1)} %broadcast_add_fusion.19, f32[64,128]{1,0:T(8,128)S(1)} %bitcast.221, f32[64,128]{1,0:T(8,128)S(1)} %broadcast_add_fusion.20, ...), kind=kOutput, calls=%fused_computation.77.clone.1 | convolution fusion | flops 57671680 | bytes 409728 | tf_op jit(solution)/shard_map/while/body/gij,kgi->kgj/dot_general | solution.py:148
  91.3 18.1 %all_to_all.68 = f32[32,2,256]{2,1,0:T(2,128)S(1)} all-to-all(f32[32,2,256]{2,1,0:T(2,128)S(1)} %copy.39), channel_id=1, replica_groups=mesh['row_0'=8,'row_1'=2,'col_0'=8,'col_1'=4] {'col_0','col_1'}, dimensions={0} | all-to-all | bytes 131072 | tf_op jit(solution)/shard_map/all_to_all | solution.py:61
  109.7 14.1 %all_to_all.69 = f32[64,1,4]{2,1,0:T(1,128)S(1)} all-to-all(f32[64,1,4]{2,1,0:T(1,128)S(1)} %broadcast_in_dim.295), channel_id=1, replica_groups=mesh['row_0'=8,'row_1'=2,'col_0'=8,'col_1'=4] {'row_1','col_0','col_1'}, dimensions={0} | all-to-all | bytes 2048 | tf_op jit(solution)/shard_map/all_to_all | solution.py:21
  123.9 0.6 broadcast_in_dim.296
  124.5 24.5 %all-to-all-start.3 = ((f32[8,1,4]{2,1,0:T(1,128)}), f32[8,1,4]{2,1,0:T(1,128)S(1)}, u32[]{:S(2)}, u32[]{:S(2)}) async-start(f32[8,1,4]{2,1,0:T(1,128)} %broadcast_in_dim.296), calls=%async_computation.3 | async-start | bytes 8192 | tf_op jit(solution)/shard_map/all_to_all | solution.py:21
  149.1 6.6 %all-to-all-done.3 = f32[8,1,4]{2,1,0:T(1,128)S(1)} async-done(((f32[8,1,4]{2,1,0:T(1,128)}), f32[8,1,4]{2,1,0:T(1,128)S(1)}, u32[]{:S(2)}, u32[]{:S(2)}) %all-to-all-start.3) | async-done | bytes 160 | tf_op jit(solution)/shard_map/all_to_all | solution.py:21
  155.8 16.5 %all_gather.14 = f32[2,4096]{1,0:T(2,128)S(1)} all-gather(f32[2,256]{1,0:T(2,128)S(1)} %multiply_subtract_fusion.1), channel_id=1, replica_groups=mesh['row_0'=8,'row_1'=2,'col_0'=8,'col_1'=4] {'row_0','row_1'}, dimensions={1}, use_global_device_ids=true | all-gather | bytes 34816 | tf_op jit(solution)/shard_map/all_gather | solution.py:144
  172.4 21.0 %while.49 = (s32[]{:T(128)}, f32[2,64,128]{2,1,0:T(8,128)S(1)}, s32[]{:T(128)}, s32[2112]{0:T(1024)S(1)}, f32[2,32,128]{2,0,1:T(2,128)S(1)}, /*index=5*/s32[]{:T...) while((s32[]{:T(128)}, f32[2,64,128]{2,1,0:T(8,128)S(1)}, ...), condition=%wide.region_19.21_spmd.clone.clone.clone, body=%wide.region_18.20_spmd.sunk.clone.clone.clone.sunk | while | flops 70322144 | bytes 2021583 | solution.py:154
  172.5 0.6 gather_fusion.9
  173.1 0.6 gather_fusion.10
  173.7 0.4 fusion.257
  174.2 0.7 gather_fusion.7
  175.2 0.8 gather_fusion.12
  176.2 0.8 gather_fusion.11
  177.0 0.7 gather_fusion.8
  177.7 0.7 gather_fusion.13
  178.4 0.6 add_compare_fusion.7
  179.0 14.2 %fusion.258 = f32[2,64,128]{2,0,1:T(2,128)S(1)} fusion(f32[64,128]{1,0:T(8,128)S(1)} %bitcast.217, f32[64,128]{1,0:T(8,128)S(1)} %bitcast.226, f32[64,128]{1,0:T(8,128)S(1)} %bitcast.224, f32[64,128]{1,0:T(8,128)S(1)} %broadcast_add_fusion.22, f32[64,128]{1,0:T(8,128)S(1)} %bitcast.225, f32[64,128]{1,0:T(8,128)S(1)} %broadcast_add_fusion.23, ...), kind=kOutput, calls=%fused_computation.161.clone.1 | convolution fusion | flops 57671680 | bytes 409728 | tf_op jit(solution)/shard_map/while/body/gij,kgi->kgj/dot_general | solution.py:148
  193.5 11.8 %all_to_all.70 = f32[32,2,256]{2,1,0:T(2,128)S(1)} all-to-all(f32[32,2,256]{2,1,0:T(2,128)S(1)} %copy.42), channel_id=1, replica_groups=mesh['row_0'=8,'row_1'=2,'col_0'=8,'col_1'=4] {'col_0','col_1'}, dimensions={0} | all-to-all | bytes 131072 | tf_op jit(solution)/shard_map/all_to_all | solution.py:61
  205.7 14.0 %all_to_all.71 = f32[64,1,4]{2,1,0:T(1,128)S(1)} all-to-all(f32[64,1,4]{2,1,0:T(1,128)S(1)} %broadcast_in_dim.297), channel_id=1, replica_groups=mesh['row_0'=8,'row_1'=2,'col_0'=8,'col_1'=4] {'row_1','col_0','col_1'}, dimensions={0} | all-to-all | bytes 2048 | tf_op jit(solution)/shard_map/all_to_all | solution.py:21
  219.7 0.6 broadcast_in_dim.298
  220.3 24.5 %all-to-all-start.6 = ((f32[8,1,4]{2,1,0:T(1,128)}), f32[8,1,4]{2,1,0:T(1,128)S(1)}, u32[]{:S(2)}, u32[]{:S(2)}) async-start(f32[8,1,4]{2,1,0:T(1,128)} %broadcast_in_dim.298), calls=%async_computation.6 | async-start | bytes 8192 | tf_op jit(solution)/shard_map/all_to_all | solution.py:21
  244.8 6.6 %all-to-all-done.6 = f32[8,1,4]{2,1,0:T(1,128)S(1)} async-done(((f32[8,1,4]{2,1,0:T(1,128)}), f32[8,1,4]{2,1,0:T(1,128)S(1)}, u32[]{:S(2)}, u32[]{:S(2)}) %all-to-all-start.6) | async-done | bytes 160 | tf_op jit(solution)/shard_map/all_to_all | solution.py:21
  251.6 16.5 %all_gather.15 = f32[2,4096]{1,0:T(2,128)S(1)} all-gather(f32[2,256]{1,0:T(2,128)S(1)} %multiply_subtract_fusion), channel_id=1, replica_groups=mesh['row_0'=8,'row_1'=2,'col_0'=8,'col_1'=4] {'row_0','row_1'}, dimensions={1}, use_global_device_ids=true | all-gather | bytes 34816 | tf_op jit(solution)/shard_map/all_gather | solution.py:144
  268.1 21.0 %while.50 = (s32[]{:T(128)}, f32[2,64,128]{2,1,0:T(8,128)S(1)}, s32[]{:T(128)}, s32[2112]{0:T(1024)S(1)}, f32[2,32,128]{2,0,1:T(2,128)S(1)}, /*index=5*/s32[]{:T...) while((s32[]{:T(128)}, f32[2,64,128]{2,1,0:T(8,128)S(1)}, ...), condition=%wide.region_26.28_spmd.clone.clone.clone, body=%wide.region_25.27_spmd.sunk.clone.clone.clone.sunk | while | flops 70322144 | bytes 2021583 | solution.py:154
  268.2 0.6 gather_fusion.16
  268.8 0.6 gather_fusion.17
  269.4 0.4 fusion.266
  270.0 0.7 gather_fusion.14
  271.0 0.8 gather_fusion.19
  271.9 0.8 gather_fusion.18
  272.7 0.7 gather_fusion.15
  273.5 0.7 gather_fusion.20
  274.1 0.6 add_compare_fusion.8
  274.7 14.2 %fusion.267 = f32[2,64,128]{2,0,1:T(2,128)S(1)} fusion(f32[64,128]{1,0:T(8,128)S(1)} %bitcast.218, f32[64,128]{1,0:T(8,128)S(1)} %bitcast.230, f32[64,128]{1,0:T(8,128)S(1)} %bitcast.228, f32[64,128]{1,0:T(8,128)S(1)} %broadcast_add_fusion.25, f32[64,128]{1,0:T(8,128)S(1)} %bitcast.229, f32[64,128]{1,0:T(8,128)S(1)} %broadcast_add_fusion.26, ...), kind=kOutput, calls=%fused_computation.245.clone.1 | convolution fusion | flops 57671680 | bytes 409728 | tf_op jit(solution)/shard_map/while/body/gij,kgi->kgj/dot_general | solution.py:148
  289.2 11.8 %all_to_all.72 = f32[32,2,256]{2,1,0:T(2,128)S(1)} all-to-all(f32[32,2,256]{2,1,0:T(2,128)S(1)} %copy.45), channel_id=1, replica_groups=mesh['row_0'=8,'row_1'=2,'col_0'=8,'col_1'=4] {'col_0','col_1'}, dimensions={0} | all-to-all | bytes 131072 | tf_op jit(solution)/shard_map/all_to_all | solution.py:61
  301.4 14.0 %all_to_all.73 = f32[64,1,4]{2,1,0:T(1,128)S(1)} all-to-all(f32[64,1,4]{2,1,0:T(1,128)S(1)} %broadcast_in_dim.299), channel_id=1, replica_groups=mesh['row_0'=8,'row_1'=2,'col_0'=8,'col_1'=4] {'row_1','col_0','col_1'}, dimensions={0} | all-to-all | bytes 2048 | tf_op jit(solution)/shard_map/all_to_all | solution.py:21
  315.5 30.9 %all_to_all.74 = f32[8,1,4]{2,1,0:T(1,128)S(1)} all-to-all(f32[8,1,4]{2,1,0:T(1,128)S(1)} %broadcast_in_dim.300), channel_id=1, replica_groups=mesh['row_0'=8,'row_1'=2,'col_0'=8,'col_1'=4] {'row_0'}, dimensions={0} | all-to-all | bytes 256 | tf_op jit(solution)/shard_map/all_to_all | solution.py:21
  346.7 14.5 %all_to_all.75 = f32[64,1,2]{2,1,0:T(1,128)S(1)} all-to-all(f32[64,1,2]{2,1,0:T(1,128)S(1)} %broadcast_in_dim.301), channel_id=1, replica_groups=mesh['row_0'=8,'row_1'=2,'col_0'=8,'col_1'=4] {'row_1','col_0','col_1'}, dimensions={0} | all-to-all | bytes 1024 | tf_op jit(solution)/shard_map/all_to_all | solution.py:21
  361.3 8.9 %all_to_all.76 = f32[8,1,2]{2,1,0:T(1,128)S(1)} all-to-all(f32[8,1,2]{2,1,0:T(1,128)S(1)} %broadcast_in_dim.302), channel_id=1, replica_groups=mesh['row_0'=8,'row_1'=2,'col_0'=8,'col_1'=4] {'row_0'}, dimensions={0} | all-to-all | bytes 128 | tf_op jit(solution)/shard_map/all_to_all | solution.py:21
  370.2 0.6 fusion.214
  372.2 0.6 fusion.204
  (120 shorter events, 7.1 us)
Async XLA Ops:
  0.0 18.2 %copy-start.3 = (s32[3,1024]{1,0:T(4,128)S(1)}, s32[3,1024]{1,0:T(4,128)}, u32[]{:S(2)}) copy-start(s32[3,1024]{1,0:T(4,128)} %param.17) | copy-start | bytes 36868
  2.2 67.9 %all-to-all-start = ((f32[32,4,256]{2,1,0:T(4,128)}), f32[32,4,256]{2,1,0:T(4,128)S(1)}, u32[]{:S(2)}, u32[]{:S(2)}) async-start(f32[32,4,256]{2,1,0:T(4,128)} %broadcast_in_dim.293), calls=%async_computation | async-start | bytes 262144 | tf_op jit(solution)/shard_map/all_to_all | solution.py:21
  18.2 51.9 %copy-start = (s32[3]{0:T(128)S(1)}, s32[3]{0:T(128)}, u32[]{:S(2)}) copy-start(s32[3]{0:T(128)} %constant.962) | copy-start | bytes 40
  18.2 51.9 %copy-start.1 = (s32[3]{0:T(128)S(1)}, s32[3]{0:T(128)}, u32[]{:S(2)}) copy-start(s32[3]{0:T(128)} %constant.963) | copy-start | bytes 40
  18.2 51.9 %copy-start.2 = (s32[3]{0:T(128)S(1)}, s32[3]{0:T(128)}, u32[]{:S(2)}) copy-start(s32[3]{0:T(128)} %constant.964) | copy-start | bytes 40
  124.5 31.1 %all-to-all-start.3 = ((f32[8,1,4]{2,1,0:T(1,128)}), f32[8,1,4]{2,1,0:T(1,128)S(1)}, u32[]{:S(2)}, u32[]{:S(2)}) async-start(f32[8,1,4]{2,1,0:T(1,128)} %broadcast_in_dim.296), calls=%async_computation.3 | async-start | bytes 8192 | tf_op jit(solution)/shard_map/all_to_all | solution.py:21
  220.3 31.1 %all-to-all-start.6 = ((f32[8,1,4]{2,1,0:T(1,128)}), f32[8,1,4]{2,1,0:T(1,128)S(1)}, u32[]{:S(2)}, u32[]{:S(2)}) async-start(f32[8,1,4]{2,1,0:T(1,128)} %broadcast_in_dim.298), calls=%async_computation.6 | async-start | bytes 8192 | tf_op jit(solution)/shard_map/all_to_all | solution.py:21
where the time goes:
time: 374 us; the launch traced here: 373 us
  blocking collectives  205 us (55%)
  starting transfers between devices  62.8 us (17%)
  matrix products  43.2 us (12%)
  other arithmetic  25.8 us (7%)
  local copies, waits for them, and re-layouts  20.5 us (5%)
  waiting for transfers between devices  13.1 us (4%)
    all_to_all x6, blocking collectives, copy_for_each(): lax.all_to_all(jnp.broadcast_to(value[None], (devices, *value.shape)), ax...  96.4 us
    all_to_all x3, starting transfers between devices, copy_for_each(): lax.all_to_all(jnp.broadcast_to(value[None], (devices, *value.shape)), ax...  62.8 us
    all_gather x3, blocking collectives, apply(): lax.all_gather(direction, ROW, axis=1, tiled=True).reshape(2, n_tgt, BLOCK)  51.5 us
    dot_general x3, matrix products, turn(): jnp.einsum('gij,kgi->kgj', kern, remote[:, tgt_blk], precision=lax.Precis...  42.6 us
    all_to_all x3, blocking collectives, sent_and_summed(): lax.all_to_all(in_blocks(value, dim, devices), axis, 0, 0, tiled=True)  41.8 us
    all_gather x1, blocking collectives, per_device(): lax.all_gather(geo, ROW, axis=1, tiled=True).reshape(4, n_tgt, BLOCK)  15.1 us
    scatter-add x1, other arithmetic, per_device(): jnp.nonzero(tile, size=n_tgt * n_src + pair_group, fill_value=0)[0]  14.7 us
    all_to_all x3, waiting for transfers between devices, copy_for_each(): lax.all_to_all(jnp.broadcast_to(value[None], (devices, *value.shape)), ax...  13.1 us
  transfers between devices with their start and end apart: 3, of which 2 were waited for; matrix products, arithmetic and copies ran while one was open for 5% of the time, Pallas kernels for 0%

commit v1 on v0

--- a/solution.py
+++ b/solution.py
@@ -141,7 +141,7 @@
         return (jnp.where(live[:, None, None], kern, 0.0), tgt_blk, src_blk)
 
     def apply(direction):
-        remote = lax.all_gather(direction, ROW, axis=1, tiled=True).reshape(2, n_tgt, BLOCK)
+        remote = jnp.concatenate(lax.all_gather(direction, ROW), axis=1).reshape(2, n_tgt, BLOCK)
 
         def turn(step, acc):
             kern, tgt_blk, src_blk = block_kernel(step)

time: 374 us -> 374 us (level)
  no operation moved by 1% of the time
where the time goes in v1:
time: 374 us; the launch traced here: 373 us
  blocking collectives  205 us (55%)
  starting transfers between devices  62.8 us (17%)
  matrix products  43.2 us (12%)
  other arithmetic  25.8 us (7%)
  local copies, waits for them, and re-layouts  20.5 us (5%)
  waiting for transfers between devices  13.1 us (4%)
    all_to_all x6, blocking collectives, copy_for_each(): lax.all_to_all(jnp.broadcast_to(value[None], (devices, *value.shape)), ax...  96.4 us
    all_to_all x3, starting transfers between devices, copy_for_each(): lax.all_to_all(jnp.broadcast_to(value[None], (devices, *value.shape)), ax...  62.8 us
    all_gather x3, blocking collectives, apply(): lax.all_gather(direction, ROW)  51.5 us
    dot_general x3, matrix products, turn(): jnp.einsum('gij,kgi->kgj', kern, remote[:, tgt_blk], precision=lax.Precis...  42.6 us
    all_to_all x3, blocking collectives, sent_and_summed(): lax.all_to_all(in_blocks(value, dim, devices), axis, 0, 0, tiled=True)  41.8 us
    all_gather x1, blocking collectives, per_device(): lax.all_gather(geo, ROW, axis=1, tiled=True).reshape(4, n_tgt, BLOCK)  15.1 us
    scatter-add x1, other arithmetic, per_device(): jnp.nonzero(tile, size=n_tgt * n_src + pair_group, fill_value=0)[0]  14.7 us
    all_to_all x3, waiting for transfers between devices, copy_for_each(): lax.all_to_all(jnp.broadcast_to(value[None], (devices, *value.shape)), ax...  13.1 us
  transfers between devices with their start and end apart: 3, of which 2 were waited for; matrix products, arithmetic and copies ran while one was open for 5% of the time, Pallas kernels for 0%

profile of v1, /device:TPU:1, one launch (start us, length us, event | category | flops | bytes accessed | tf_op | source)
XLA Modules:
  0.0 372.8 jit_solution(16744334833945063564)
XLA Ops:
  0.0 0.8 select_reduce_fusion
  0.8 0.7 pad_maximum_fusion
  1.5 0.7 broadcast_in_dim.293
  2.2 13.7 %all-to-all-start = ((f32[32,4,256]{2,1,0:T(4,128)}), f32[32,4,256]{2,1,0:T(4,128)S(1)}, u32[]{:S(2)}, u32[]{:S(2)}) async-start(f32[32,4,256]{2,1,0:T(4,128)} %broadcast_in_dim.293), calls=%async_computation | async-start | bytes 262144 | tf_op jit(solution)/shard_map/all_to_all | solution.py:21
  15.9 1.4 fusion.201
  18.5 0.6 gather_fusion.21
  19.1 0.6 gather_fusion.22
  19.8 0.3 reduce-window.16
  20.4 14.7 %scatter_custom_fusion = s32[2112]{0:T(1024)S(1)} fusion(s32[2048]{0:T(1024)S(1)} %bitcast.253, s32[2048]{0:T(1024)S(1)} %broadcast.958, s32[]{:T(128)} %constant.520.clone.1), kind=kCustom, calls=%fused_computation.302 | custom fusion | flops 2048 | bytes 8452 | tf_op jit(solution)/shard_map/scatter-add | solution.py:124
  35.7 18.5 %all-gather.3 = f32[16,2,256]{2,1,0:T(2,128)S(1)} all-gather(f32[1,2,256]{2,1,0:T(2,128)S(1)} %pad_bitcast_fusion.1), channel_id=2, replica_groups=mesh['row_0'=8,'row_1'=2,'col_0'=8,'col_1'=4] {'row_0','row_1'}, dimensions={0}, use_global_device_ids=true | all-gather | bytes 34816 | tf_op jit(solution)/shard_map/all_gather | solution.py:144
  54.2 0.7 fusion.199
  54.9 15.1 %all_gather.23 = f32[4,4096]{1,0:T(4,128)S(1)} all-gather(f32[4,256]{1,0:T(4,128)S(1)} %pad_maximum_fusion), channel_id=1, replica_groups=mesh['row_0'=8,'row_1'=2,'col_0'=8,'col_1'=4] {'row_0','row_1'}, dimensions={1}, use_global_device_ids=true | all-gather | bytes 69632 | tf_op jit(solution)/shard_map/all_gather | solution.py:114
  70.1 21.0 %while.48 = (s32[]{:T(128)}, f32[2,64,128]{2,1,0:T(8,128)S(1)}, s32[]{:T(128)}, s32[2112]{0:T(1024)S(1)}, f32[2,32,128]{2,0,1:T(2,128)S(1)}, /*index=5*/s32[]{:T...) while((s32[]{:T(128)}, f32[2,64,128]{2,1,0:T(8,128)S(1)}, ...), condition=%wide.region_11.13_spmd.clone.clone.clone, body=%wide.region_10.12_spmd.sunk.clone.clone.clone.sunk | while | flops 70322144 | bytes 2021583 | solution.py:154
  70.3 0.6 gather_fusion.2
  70.9 0.6 gather_fusion.3
  71.5 0.4 fusion.256
  72.0 0.7 gather_fusion
  73.0 0.8 gather_fusion.5
  74.0 0.8 gather_fusion.4
  74.8 0.7 gather_fusion.1
  75.5 0.7 gather_fusion.6
  76.2 0.6 add_compare_fusion.6
  76.8 14.2 %fusion.257 = f32[2,64,128]{2,0,1:T(2,128)S(1)} fusion(f32[64,128]{1,0:T(8,128)S(1)} %bitcast.227, f32[64,128]{1,0:T(8,128)S(1)} %bitcast.233, f32[64,128]{1,0:T(8,128)S(1)} %bitcast.231, f32[64,128]{1,0:T(8,128)S(1)} %broadcast_add_fusion.19, f32[64,128]{1,0:T(8,128)S(1)} %bitcast.232, f32[64,128]{1,0:T(8,128)S(1)} %broadcast_add_fusion.20, ...), kind=kOutput, calls=%fused_computation.77.clone.1 | convolution fusion | flops 57671680 | bytes 409728 | tf_op jit(solution)/shard_map/while/body/gij,kgi->kgj/dot_general | solution.py:148
  91.3 18.1 %all_to_all.68 = f32[32,2,256]{2,1,0:T(2,128)S(1)} all-to-all(f32[32,2,256]{2,1,0:T(2,128)S(1)} %copy.41), channel_id=1, replica_groups=mesh['row_0'=8,'row_1'=2,'col_0'=8,'col_1'=4] {'col_0','col_1'}, dimensions={0} | all-to-all | bytes 131072 | tf_op jit(solution)/shard_map/all_to_all | solution.py:61
  109.7 14.1 %all_to_all.69 = f32[64,1,4]{2,1,0:T(1,128)S(1)} all-to-all(f32[64,1,4]{2,1,0:T(1,128)S(1)} %broadcast_in_dim.295), channel_id=1, replica_groups=mesh['row_0'=8,'row_1'=2,'col_0'=8,'col_1'=4] {'row_1','col_0','col_1'}, dimensions={0} | all-to-all | bytes 2048 | tf_op jit(solution)/shard_map/all_to_all | solution.py:21
  123.9 0.6 broadcast_in_dim.296
  124.5 24.5 %all-to-all-start.3 = ((f32[8,1,4]{2,1,0:T(1,128)}), f32[8,1,4]{2,1,0:T(1,128)S(1)}, u32[]{:S(2)}, u32[]{:S(2)}) async-start(f32[8,1,4]{2,1,0:T(1,128)} %broadcast_in_dim.296), calls=%async_computation.3 | async-start | bytes 8192 | tf_op jit(solution)/shard_map/all_to_all | solution.py:21
  149.1 6.6 %all-to-all-done.3 = f32[8,1,4]{2,1,0:T(1,128)S(1)} async-done(((f32[8,1,4]{2,1,0:T(1,128)}), f32[8,1,4]{2,1,0:T(1,128)S(1)}, u32[]{:S(2)}, u32[]{:S(2)}) %all-to-all-start.3) | async-done | bytes 160 | tf_op jit(solution)/shard_map/all_to_all | solution.py:21
  155.8 16.5 %all-gather.4 = f32[16,2,256]{2,1,0:T(2,128)S(1)} all-gather(f32[1,2,256]{2,1,0:T(2,128)S(1)} %fusion.222), channel_id=3, replica_groups=mesh['row_0'=8,'row_1'=2,'col_0'=8,'col_1'=4] {'row_0','row_1'}, dimensions={0}, use_global_device_ids=true | all-gather | bytes 34816 | tf_op jit(solution)/shard_map/all_gather | solution.py:144
  172.4 21.0 %while.49 = (s32[]{:T(128)}, f32[2,64,128]{2,1,0:T(8,128)S(1)}, s32[]{:T(128)}, s32[2112]{0:T(1024)S(1)}, f32[2,32,128]{2,0,1:T(2,128)S(1)}, /*index=5*/s32[]{:T...) while((s32[]{:T(128)}, f32[2,64,128]{2,1,0:T(8,128)S(1)}, ...), condition=%wide.region_19.21_spmd.clone.clone.clone, body=%wide.region_18.20_spmd.sunk.clone.clone.clone.sunk | while | flops 70322144 | bytes 2021583 | solution.py:154
  172.5 0.6 gather_fusion.9
  173.1 0.6 gather_fusion.10
  173.7 0.4 fusion.265
  174.2 0.7 gather_fusion.7
  175.2 0.8 gather_fusion.12
  176.2 0.8 gather_fusion.11
  177.0 0.7 gather_fusion.8
  177.7 0.7 gather_fusion.13
  178.4 0.6 add_compare_fusion.7
  179.0 14.2 %fusion.266 = f32[2,64,128]{2,0,1:T(2,128)S(1)} fusion(f32[64,128]{1,0:T(8,128)S(1)} %bitcast.228, f32[64,128]{1,0:T(8,128)S(1)} %bitcast.237, f32[64,128]{1,0:T(8,128)S(1)} %bitcast.235, f32[64,128]{1,0:T(8,128)S(1)} %broadcast_add_fusion.22, f32[64,128]{1,0:T(8,128)S(1)} %bitcast.236, f32[64,128]{1,0:T(8,128)S(1)} %broadcast_add_fusion.23, ...), kind=kOutput, calls=%fused_computation.161.clone.1 | convolution fusion | flops 57671680 | bytes 409728 | tf_op jit(solution)/shard_map/while/body/gij,kgi->kgj/dot_general | solution.py:148
  193.5 11.8 %all_to_all.70 = f32[32,2,256]{2,1,0:T(2,128)S(1)} all-to-all(f32[32,2,256]{2,1,0:T(2,128)S(1)} %copy.44), channel_id=1, replica_groups=mesh['row_0'=8,'row_1'=2,'col_0'=8,'col_1'=4] {'col_0','col_1'}, dimensions={0} | all-to-all | bytes 131072 | tf_op jit(solution)/shard_map/all_to_all | solution.py:61
  205.7 14.0 %all_to_all.71 = f32[64,1,4]{2,1,0:T(1,128)S(1)} all-to-all(f32[64,1,4]{2,1,0:T(1,128)S(1)} %broadcast_in_dim.297), channel_id=1, replica_groups=mesh['row_0'=8,'row_1'=2,'col_0'=8,'col_1'=4] {'row_1','col_0','col_1'}, dimensions={0} | all-to-all | bytes 2048 | tf_op jit(solution)/shard_map/all_to_all | solution.py:21
  219.7 0.6 broadcast_in_dim.298
  220.3 24.5 %all-to-all-start.6 = ((f32[8,1,4]{2,1,0:T(1,128)}), f32[8,1,4]{2,1,0:T(1,128)S(1)}, u32[]{:S(2)}, u32[]{:S(2)}) async-start(f32[8,1,4]{2,1,0:T(1,128)} %broadcast_in_dim.298), calls=%async_computation.6 | async-start | bytes 8192 | tf_op jit(solution)/shard_map/all_to_all | solution.py:21
  244.8 6.6 %all-to-all-done.6 = f32[8,1,4]{2,1,0:T(1,128)S(1)} async-done(((f32[8,1,4]{2,1,0:T(1,128)}), f32[8,1,4]{2,1,0:T(1,128)S(1)}, u32[]{:S(2)}, u32[]{:S(2)}) %all-to-all-start.6) | async-done | bytes 160 | tf_op jit(solution)/shard_map/all_to_all | solution.py:21
  251.6 16.5 %all-gather.5 = f32[16,2,256]{2,1,0:T(2,128)S(1)} all-gather(f32[1,2,256]{2,1,0:T(2,128)S(1)} %bitcast.251), channel_id=4, replica_groups=mesh['row_0'=8,'row_1'=2,'col_0'=8,'col_1'=4] {'row_0','row_1'}, dimensions={0}, use_global_device_ids=true | all-gather | bytes 34816 | tf_op jit(solution)/shard_map/all_gather | solution.py:144
  268.1 21.0 %while.50 = (s32[]{:T(128)}, f32[2,64,128]{2,1,0:T(8,128)S(1)}, s32[]{:T(128)}, s32[2112]{0:T(1024)S(1)}, f32[2,32,128]{2,0,1:T(2,128)S(1)}, /*index=5*/s32[]{:T...) while((s32[]{:T(128)}, f32[2,64,128]{2,1,0:T(8,128)S(1)}, ...), condition=%wide.region_26.28_spmd.clone.clone.clone, body=%wide.region_25.27_spmd.sunk.clone.clone.clone.sunk | while | flops 70322144 | bytes 2021583 | solution.py:154
  268.2 0.6 gather_fusion.16
  268.8 0.6 gather_fusion.17
  269.4 0.4 fusion.274
  270.0 0.7 gather_fusion.14
  271.0 0.8 gather_fusion.19
  271.9 0.8 gather_fusion.18
  272.7 0.7 gather_fusion.15
  273.5 0.7 gather_fusion.20
  274.1 0.6 add_compare_fusion.8
  274.7 14.2 %fusion.275 = f32[2,64,128]{2,0,1:T(2,128)S(1)} fusion(f32[64,128]{1,0:T(8,128)S(1)} %bitcast.229, f32[64,128]{1,0:T(8,128)S(1)} %bitcast.241, f32[64,128]{1,0:T(8,128)S(1)} %bitcast.239, f32[64,128]{1,0:T(8,128)S(1)} %broadcast_add_fusion.25, f32[64,128]{1,0:T(8,128)S(1)} %bitcast.240, f32[64,128]{1,0:T(8,128)S(1)} %broadcast_add_fusion.26, ...), kind=kOutput, calls=%fused_computation.245.clone.1 | convolution fusion | flops 57671680 | bytes 409728 | tf_op jit(solution)/shard_map/while/body/gij,kgi->kgj/dot_general | solution.py:148
  289.2 11.8 %all_to_all.72 = f32[32,2,256]{2,1,0:T(2,128)S(1)} all-to-all(f32[32,2,256]{2,1,0:T(2,128)S(1)} %copy.47), channel_id=1, replica_groups=mesh['row_0'=8,'row_1'=2,'col_0'=8,'col_1'=4] {'col_0','col_1'}, dimensions={0} | all-to-all | bytes 131072 | tf_op jit(solution)/shard_map/all_to_all | solution.py:61
  301.4 14.0 %all_to_all.73 = f32[64,1,4]{2,1,0:T(1,128)S(1)} all-to-all(f32[64,1,4]{2,1,0:T(1,128)S(1)} %broadcast_in_dim.299), channel_id=1, replica_groups=mesh['row_0'=8,'row_1'=2,'col_0'=8,'col_1'=4] {'row_1','col_0','col_1'}, dimensions={0} | all-to-all | bytes 2048 | tf_op jit(solution)/shard_map/all_to_all | solution.py:21
  315.5 30.9 %all_to_all.74 = f32[8,1,4]{2,1,0:T(1,128)S(1)} all-to-all(f32[8,1,4]{2,1,0:T(1,128)S(1)} %broadcast_in_dim.300), channel_id=1, replica_groups=mesh['row_0'=8,'row_1'=2,'col_0'=8,'col_1'=4] {'row_0'}, dimensions={0} | all-to-all | bytes 256 | tf_op jit(solution)/shard_map/all_to_all | solution.py:21
  346.7 14.5 %all_to_all.75 = f32[64,1,2]{2,1,0:T(1,128)S(1)} all-to-all(f32[64,1,2]{2,1,0:T(1,128)S(1)} %broadcast_in_dim.301), channel_id=1, replica_groups=mesh['row_0'=8,'row_1'=2,'col_0'=8,'col_1'=4] {'row_1','col_0','col_1'}, dimensions={0} | all-to-all | bytes 1024 | tf_op jit(solution)/shard_map/all_to_all | solution.py:21
  361.3 8.9 %all_to_all.76 = f32[8,1,2]{2,1,0:T(1,128)S(1)} all-to-all(f32[8,1,2]{2,1,0:T(1,128)S(1)} %broadcast_in_dim.302), channel_id=1, replica_groups=mesh['row_0'=8,'row_1'=2,'col_0'=8,'col_1'=4] {'row_0'}, dimensions={0} | all-to-all | bytes 128 | tf_op jit(solution)/shard_map/all_to_all | solution.py:21
  370.2 0.6 fusion.221
  372.2 0.6 fusion.210
  (120 shorter events, 7.1 us)
Async XLA Ops:
  0.0 18.2 %copy-start.3 = (s32[3,1024]{1,0:T(4,128)S(1)}, s32[3,1024]{1,0:T(4,128)}, u32[]{:S(2)}) copy-start(s32[3,1024]{1,0:T(4,128)} %param.17) | copy-start | bytes 36868
  2.2 67.9 %all-to-all-start = ((f32[32,4,256]{2,1,0:T(4,128)}), f32[32,4,256]{2,1,0:T(4,128)S(1)}, u32[]{:S(2)}, u32[]{:S(2)}) async-start(f32[32,4,256]{2,1,0:T(4,128)} %broadcast_in_dim.293), calls=%async_computation | async-start | bytes 262144 | tf_op jit(solution)/shard_map/all_to_all | solution.py:21
  18.2 51.9 %copy-start = (s32[3]{0:T(128)S(1)}, s32[3]{0:T(128)}, u32[]{:S(2)}) copy-start(s32[3]{0:T(128)} %constant.970) | copy-start | bytes 40
  18.2 51.9 %copy-start.1 = (s32[3]{0:T(128)S(1)}, s32[3]{0:T(128)}, u32[]{:S(2)}) copy-start(s32[3]{0:T(128)} %constant.971) | copy-start | bytes 40
  18.2 51.9 %copy-start.2 = (s32[3]{0:T(128)S(1)}, s32[3]{0:T(128)}, u32[]{:S(2)}) copy-start(s32[3]{0:T(128)} %constant.972) | copy-start | bytes 40
  124.5 31.1 %all-to-all-start.3 = ((f32[8,1,4]{2,1,0:T(1,128)}), f32[8,1,4]{2,1,0:T(1,128)S(1)}, u32[]{:S(2)}, u32[]{:S(2)}) async-start(f32[8,1,4]{2,1,0:T(1,128)} %broadcast_in_dim.296), calls=%async_computation.3 | async-start | bytes 8192 | tf_op jit(solution)/shard_map/all_to_all | solution.py:21
  220.3 31.1 %all-to-all-start.6 = ((f32[8,1,4]{2,1,0:T(1,128)}), f32[8,1,4]{2,1,0:T(1,128)S(1)}, u32[]{:S(2)}, u32[]{:S(2)}) async-start(f32[8,1,4]{2,1,0:T(1,128)} %broadcast_in_dim.298), calls=%async_computation.6 | async-start | bytes 8192 | tf_op jit(solution)/shard_map/all_to_all | solution.py:21
